TPU v7x, 128 devices: a whole 4x4x4 slice. The times are simulated.
128 devices in a mesh: leaf: 128 (over x, z, y, core).
Axes of the slice: x: 4, y: 4, z: 4, core: 2. Of those that a mesh axis runs over, the one named last changes fastest.
Arguments:
- slip: bfloat16 [128, 32768], P(None, 'leaf'), may hold values from -6 to 6
- to_multipole: bfloat16 [121, 128], replicated, may hold values from -0.5 to 0.5
- up_shift: float32 [2, 121, 121], replicated, may hold values from -0.375 to 0.375
- down_shift: float32 [2, 121, 121], replicated, may hold values from -0.5 to 0.5
- sibling_far: float32 [2, 121, 121], replicated, may hold values from -0.5 to 0.5
- leaf_far: bfloat16 [27, 121, 121], replicated, may hold values from -0.25 to 0.25
- to_stress: bfloat16 [128, 121], replicated, may hold values from -0.125 to 0.125
- near_blocks: bfloat16 [9, 128, 128], replicated, may hold values from -0.1875 to 0.1875
- send_cells: int32 [128, 16384], P('leaf'), may hold values from 0 to 255, as said below
- far_list: int32 [27, 32768], P(None, 'leaf'), may hold values from 0 to 16639, as said below
- near_list: int32 [9, 32768], P(None, 'leaf'), may hold values from 0 to 319, as said below
Outputs:
- stress: float32 [128, 32768], P(None, 'leaf')
Inputs may be any that keep to these rules, and one draw needn't show every extreme that they name: `send_cells`: row q holds, in positions d * 128 to (d + 1) * 128 - 1, 128 distinct cells of device q (numbered within that device) listed for receiving device d. `far_list`: an entry v below 256 names a cell of the target's own device. Otherwise v - 256 = q * 128 + s names slot s of device q's list for the target's device, q is not the target's device, s < 128 when q lies within 4 devices of it and s < 32 when it lies farther; in every draw some entry names slot 127 of a device within 4, and some names slot 31 of a farther device. `near_list`: an entry w names the cell w - 32 counted from the first cell of the target's device, so that positions before 0 and from 256 on lie on the neighbouring devices (zeros outside the fault); entry 4 is the target itself.
All inputs are finite; a program needn't handle non-finite values.
Results may differ from a plain program's by a relative error of at most 0.0031.
Values may be sent and summed in bfloat16 or wider, within the bound.
No kernel may reach another device: no remote copies, remote signals or barrier semaphores. Data moves between devices by JAX's collectives and lax.ppermute only.
A program may use at most 64 MiB of HBM per device.

v0:
```python
import jax
import jax.numpy as jnp
from jax import lax
from jax.experimental import pallas as pl
from jax.experimental.pallas import tpu as pltpu
from jax.sharding import PartitionSpec as P


NEAR = 9
TYPES = 27
HALO = 32
CAP_NEAR = 128
CAP_FAR = 32
EXTRA = CAP_NEAR - CAP_FAR
LANES = 128
TRIPLE = 3 * LANES
GROUP = 8
MIX = 100
OFFSETS = (-1, 1, -3, -4, -2, 3, 4, 2)

VM = pl.BlockSpec(memory_space=pltpu.VMEM)
SM = pl.BlockSpec(memory_space=pltpu.SMEM)
F32 = jnp.float32
BF16 = jnp.bfloat16
NT = (((1,), (1,)), ((), ()))
NN = (((1,), (0,)), ((), ()))


def iota(dims, dim):
    return lax.broadcasted_iota(jnp.int32, dims, dim)


def reversed_bits(value, bits):
    out = 0
    for bit in range(bits):
        out = out | ((value >> bit) & 1) << (bits - 1 - bit)
    return out


def bdot(a, b, dims):
    return lax.dot_general(a, b, dims, preferred_element_type=F32)


def one_hot(column, row):
    return jnp.where(column == row, 1.0, 0.0).astype(BF16)


def halves(x):
    high = x.astype(BF16)
    return high, (x - high.astype(F32)).astype(BF16)


def tripled(x):
    high, low = halves(x)
    return [high, high, low]


def lanes(parts):
    return jnp.concatenate(parts, axis=1)


def rows(parts):
    return jnp.concatenate(parts, axis=0)


def put_split(ref, at, block, square):
    square[: block.shape[0], : block.shape[1]] = block
    high, low = halves(square[...])
    for part, value in enumerate((high, low, high)):
        start = at + part * LANES
        ref[:, start : start + LANES] = value


def bit_order(size, bits):
    inner = reversed_bits(iota((8, size), 0), 3) << (bits - 3)
    gap = iota((8, size), 1) - inner
    blocks = [
        jnp.where(gap == reversed_bits(block, bits - 3), 1.0, 0.0) for block in range(size // 8)
    ]
    return rows(blocks).astype(BF16)


def matches(picked, spare, cells):
    at = iota((LANES, cells), 0)
    return jnp.where(
        at == spare, -iota((LANES, cells), 1).astype(F32), jnp.where(picked(at), 1.0, 0.0)
    ).astype(BF16)


def send_kernel(own, slip, to_mult, up_shift, send, far_out, up_out, down_out, plus_out,
                minus_out, mult_out, slip_out, agg_out, wu, tm, lists, square):
    cells = slip.shape[1]
    coef = to_mult.shape[0]
    devices = send.shape[0]
    bits = cells.bit_length() - 1
    tm[...] = jnp.zeros_like(tm)
    tm[:coef, :] = to_mult[...]
    square[...] = jnp.zeros_like(square)
    put_split(wu, 0, up_shift[:, 0, :], square)
    put_split(wu, TRIPLE, up_shift[:, 1, :], square)
    unit = one_hot(iota((cells, cells), 0), iota((cells, cells), 1))
    slip_rows = bdot(unit, slip[...], NT).astype(BF16)
    slip_out[...] = slip_rows
    mult = bdot(slip_rows, tm[...], NT).astype(BF16)
    mult_out[...] = mult
    lists[...] = send[...].astype(F32)
    level = bdot(bit_order(cells, bits), mult, NN)
    start, size = 0, cells
    for _ in range(bits):
        agg_out[start : start + size, :] = level
        start += size
        size //= 2
        level = bdot(lanes(tripled(level[:size]) + tripled(level[size:])), wu[...], NT)
    spread = one_hot(iota((LANES, LANES), 0) % 4 + coef, iota((LANES, LANES), 1))
    own_row = (iota((CAP_FAR, LANES), 1) // 4) == iota((CAP_FAR, LANES), 0)
    placed = jnp.where(own_row, level, 0.0).astype(BF16)
    tail = rows([bdot(placed, spread, NN)] * GROUP)
    lane = iota((CAP_FAR, LANES), 1)
    own_slot = lane == iota((CAP_FAR, LANES), 0)
    rest = jnp.where(lane == CAP_FAR, 1.0, 0.0)
    far_match = matches(lambda at: at < CAP_FAR, CAP_FAR, cells)
    cell_row = iota((CAP_FAR, cells), 1).astype(F32)
    turned = lists[...].T
    for first in range(0, devices, GROUP):
        group = range(first, first + GROUP)
        if first // GROUP % MIX == 0:
            hot = rows([one_hot(turned[:CAP_FAR, d : d + 1], cell_row) for d in group])
        else:
            spots = rows([jnp.where(own_slot, lists[d : d + 1, :], rest) for d in group])
            hot = one_hot(bdot(spots.astype(BF16), far_match, NN), 0.0)
        far_out[first : first + GROUP] = (
            (bdot(hot, mult, NN) + tail).astype(BF16).reshape(GROUP, CAP_FAR, LANES)
        )
    lane = iota((EXTRA, LANES), 1)
    own_slot = lane == iota((EXTRA, LANES), 0) + CAP_FAR
    rest = jnp.where(lane == 0, 1.0, 0.0)
    near_match = matches(lambda at: at >= CAP_FAR, 0, cells)
    homes = [(up_out, 0, 1), (up_out, 1, 4), (up_out, 2, -2), (down_out, 0, -1),
             (down_out, 1, -4), (down_out, 2, 2), (plus_out, 0, 3), (minus_out, 0, -3)]
    for ref, place, step in homes:
        dest = (own[0] + step) & (devices - 1)
        spots = jnp.where(own_slot, lists[pl.ds(dest, 1), :], rest).astype(BF16)
        hot = one_hot(bdot(spots, near_match, NN), 0.0)
        ref[place * EXTRA : (place + 1) * EXTRA, :] = bdot(hot, mult, NN).astype(BF16)
    up_out[3 * EXTRA :, :] = slip_rows[cells - HALO :]
    down_out[3 * EXTRA :, :] = slip_rows[:HALO]


def tree_kernel(own, far_list, agg, down_shift, sibling, index_out, local_out, w0, w1, square):
    cells = far_list.shape[1]
    kinds = far_list.shape[0]
    bits = cells.bit_length() - 1
    devices = LANES
    value = far_list[...]
    relative = value - cells
    sender = relative >> 7
    position = relative & (CAP_NEAR - 1)
    apart = sender - own[0]
    slot = jnp.zeros_like(value)
    for place, offset in enumerate(OFFSETS):
        slot = jnp.where(apart == offset, place, slot)
    far_at = cells + sender * CAP_FAR + position
    near_at = cells + devices * CAP_FAR + slot * EXTRA + position - CAP_FAR
    mapped = jnp.where(value < cells, value, jnp.where(position < CAP_FAR, far_at, near_at))
    for part in range(cells // LANES):
        index_out[pl.ds(part, kinds, stride=cells // LANES), :] = mapped[
            :, part * LANES : (part + 1) * LANES
        ]
    square[...] = jnp.zeros_like(square)
    for ref, which in ((w0, 0), (w1, 1)):
        put_split(ref, 0, down_shift[:, which, :], square)
        put_split(ref, TRIPLE, sibling[:, which, :], square)
    starts = [0]
    for height in range(bits):
        starts.append(starts[-1] + (cells >> height))
    local = None
    for height in reversed(range(bits)):
        parts = []
        for which, weights in ((0, w0), (1, w1)):
            total = None
            if local is not None:
                total = bdot(lanes(tripled(local)), weights[:, :TRIPLE], NT)
            if height >= 1:
                half = cells >> (height + 1)
                at = starts[height] + (1 - which) * half
                other = bdot(
                    lanes(tripled(agg[at : at + half, :])), weights[:, TRIPLE:], NT
                )
                total = other if total is None else total + other
            parts.append(total)
        local = rows(parts)
    local_out[...] = local


def near_kernel(own, slip_rows, low, high, lists, blocks, out, ext, columns):
    cells, elems = slip_rows.shape
    last = LANES - 1
    ext[...] = jnp.zeros_like(ext)
    ext[:HALO, :] = jnp.where(own[0] == 0, 0.0, low[3 * EXTRA :, :].astype(F32)).astype(BF16)
    ext[HALO : HALO + cells, :] = slip_rows[...]
    ext[HALO + cells : 2 * HALO + cells, :] = jnp.where(
        own[0] == last, 0.0, high[3 * EXTRA :, :].astype(F32)
    ).astype(BF16)
    columns[...] = jnp.zeros_like(columns)
    columns[: lists.shape[0], :] = lists[...].astype(F32)
    turned = columns[...].T
    at_lane = iota((cells, ext.shape[0]), 1).astype(F32)
    total = jnp.zeros((cells, elems), F32)
    for kind in range(NEAR):
        hot = one_hot(turned[:, kind : kind + 1], at_lane)
        gathered = bdot(hot, ext[...], NN).astype(BF16)
        total = total + bdot(gathered, blocks[kind], NT)
    out[...] = total.T


def top_levels(own, far, wu, w0, w1, levels, coef, bits, tree_bits, result):
    devices = far.shape[0]
    spread = one_hot(iota((LANES, LANES), 0), iota((LANES, LANES), 1) % 4 + coef)
    keep = (iota((CAP_FAR, LANES), 1) // 4 == iota((CAP_FAR, LANES), 0)) & (
        iota((CAP_FAR, LANES), 1) < coef
    )
    roots = bdot(far[...].reshape(devices * CAP_FAR, LANES), spread, NN)
    roots = roots.reshape(devices, CAP_FAR, LANES)
    roots = jnp.sum(jnp.where(keep[None], roots, 0.0), axis=1).astype(BF16)
    level = bdot(bit_order(devices, tree_bits), roots, NN)
    yield
    start, size = 0, devices
    starts = []
    for depth in range(tree_bits):
        levels[start : start + size, :] = level
        starts.append(start)
        start += size
        size //= 2
        if depth + 1 < tree_bits:
            level = bdot(lanes(tripled(level[:size]) + tripled(level[size:])), wu[...], NT)
            yield
    local = jnp.zeros((1, LANES), F32)
    for depth in reversed(range(tree_bits)):
        node = own[0] >> depth
        place = starts[depth] + reversed_bits(node ^ 1, tree_bits - depth)
        other = levels[pl.ds(place, 1), :]
        stacked = lanes(tripled(local) + tripled(other))
        first = bdot(stacked, w0[...], NT)
        second = bdot(stacked, w1[...], NT)
        local = jnp.where((node & 1) == 0, first, second)
        yield
    for step in range(bits):
        stacked = lanes(tripled(local))
        local = rows([bdot(stacked, w0[:, :TRIPLE], NT), bdot(stacked, w1[:, :TRIPLE], NT)])
        if step + 1 == bits:
            result.append(local)
        yield


def leaf_kernel(own, index_rows, far, low, high, plus, minus, mult, wu, w0, w1, leaf_far,
                to_stress, local_own, near_part, out, index, arrived, table, levels, ts,
                *buffers):
    devices = far.shape[0]
    cells = mult.shape[0]
    coef = leaf_far.shape[1]
    bits = cells.bit_length() - 1
    tree_bits = devices.bit_length() - 1
    load = pltpu.make_async_copy(index_rows, index, arrived)
    load.start()
    ts[...] = jnp.zeros_like(ts)
    ts[:, :coef] = to_stress[...]
    table[:cells, :] = mult[...].astype(F32)
    step = 8
    for first in range(0, devices, step):
        table[cells + first * CAP_FAR : cells + (first + step) * CAP_FAR, :] = (
            far[first : first + step].reshape(step * CAP_FAR, LANES).astype(F32)
        )
    at = cells + devices * CAP_FAR
    for block in (low[:EXTRA, :], high[:EXTRA, :], plus[...], minus[...]):
        table[at : at + block.shape[0], :] = block.astype(F32)
        at += block.shape[0]

    load.wait()
    result = []
    tree = top_levels(own, far, wu, w0, w1, levels, coef, bits, tree_bits, result)
    count = len(buffers)
    total = local_own[:, :coef]
    for kind in range(TYPES):
        buffer = buffers[kind % count]
        for cell in range(cells):
            spot = kind * cells + cell
            row = index[spot // LANES, spot % LANES]
            spot = reversed_bits(cell, bits)
            buffer[spot : spot + 1, :] = table[pl.ds(row, 1), :]
        total = total + bdot(buffer[...].astype(BF16)[:, :coef], leaf_far[kind], NT)
        next(tree, None)
    total = total + result[0][:, :coef]
    expansion = bdot(bit_order(cells, bits), total.astype(BF16), NN).astype(BF16)
    out[...] = bdot(ts[:, :coef], expansion, NT) + near_part[...]


def shape(dims, dtype):
    return jax.ShapeDtypeStruct(dims, dtype)


def kept(dims, dtype):
    return pltpu.VMEM(dims, dtype)


def held(x):
    return pltpu.with_memory_space_constraint(x, pltpu.VMEM)


def limits(mib):
    return pltpu.CompilerParams(vmem_limit_bytes=mib << 20)


def scratch(dims, dtype):
    return pltpu.VMEM(dims, dtype)


def cost(flops):
    return pl.CostEstimate(flops=flops, bytes_accessed=10**6, transcendentals=0)


def shifted(block, by):
    count = lax.axis_size("leaf")
    return lax.ppermute(block, "leaf", [(i, (i + by) % count) for i in range(count)])


def body(
    slip,
    to_multipole,
    up_shift,
    down_shift,
    sibling_far,
    leaf_far,
    to_stress,
    near_blocks,
    send_cells,
    far_list,
    near_list,
):
    elems, cells = slip.shape
    devices = lax.axis_size("leaf")
    own = lax.axis_index("leaf").astype(jnp.int32).reshape(1)
    up_t, down_t, sibling_t = (
        jnp.transpose(w, (1, 0, 2)) for w in (up_shift, down_shift, sibling_far)
    )
    bundle = 3 * EXTRA + HALO
    far_send, up_send, down_send, plus_own, minus_own, mult, slip_rows, agg, wu = pl.pallas_call(
        send_kernel,
        out_shape=[
            kept((devices, CAP_FAR, LANES), BF16),
            kept((bundle, LANES), BF16),
            kept((bundle, LANES), BF16),
            kept((EXTRA, LANES), BF16),
            kept((EXTRA, LANES), BF16),
            kept((cells, LANES), BF16),
            kept((cells, elems), BF16),
            kept((2 * cells, LANES), F32),
            kept((LANES, 2 * TRIPLE), BF16),
        ],
        in_specs=[SM, VM, VM, VM, VM],
        out_specs=[VM] * 9,
        scratch_shapes=[
            scratch((LANES, elems), BF16),
            scratch((devices, CAP_NEAR), F32),
            scratch((LANES, LANES), F32),
        ],
        name="send",
    )(own, slip, to_multipole, up_t, send_cells.reshape(devices, CAP_NEAR))
    low = shifted(up_send, 1)
    high = shifted(down_send, -1)
    far = lax.all_to_all(far_send, "leaf", split_axis=0, concat_axis=0, tiled=True)
    plus = shifted(
        rows([plus_own, low[EXTRA : 2 * EXTRA], high[2 * EXTRA : 3 * EXTRA]]), 3
    )
    minus = shifted(
        rows([minus_own, high[EXTRA : 2 * EXTRA], low[2 * EXTRA : 3 * EXTRA]]), -3
    )
    index_rows = (TYPES * cells // LANES + 7) // 8 * 8
    index, local_own, w0, w1 = pl.pallas_call(
        tree_kernel,
        out_shape=[
            kept((index_rows, LANES), jnp.int32),
            kept((cells, LANES), F32),
            kept((LANES, 2 * TRIPLE), BF16),
            kept((LANES, 2 * TRIPLE), BF16),
        ],
        in_specs=[SM, VM, VM, VM, VM],
        out_specs=[VM] * 4,
        scratch_shapes=[scratch((LANES, LANES), F32)],
        cost_estimate=cost(10**9),
        compiler_params=limits(16),
        name="tree",
    )(own, far_list, held(agg), down_t, sibling_t)
    near_part = pl.pallas_call(
        near_kernel,
        out_shape=kept((elems, cells), F32),
        in_specs=[SM] + [VM] * 5,
        out_specs=VM,
        scratch_shapes=[scratch((TRIPLE, elems), BF16), scratch((LANES, cells), F32)],
        cost_estimate=cost(10**9),
        compiler_params=limits(16),
        name="near",
    )(own, held(slip_rows), held(low), held(high), near_list, held(near_blocks))
    table_rows = cells + devices * CAP_FAR + len(OFFSETS) * EXTRA
    return pl.pallas_call(
        leaf_kernel,
        out_shape=shape((elems, cells), F32),
        in_specs=[SM] + [VM] * 14,
        out_specs=VM,
        scratch_shapes=[
            pltpu.SMEM((index_rows, LANES), jnp.int32),
            pltpu.SemaphoreType.DMA,
            scratch((table_rows, LANES), F32),
            scratch((2 * devices, LANES), F32),
            scratch((elems, LANES), BF16),
        ]
        + [scratch((cells, LANES), F32)] * 6,
        compiler_params=limits(24),
        name="leaf",
    )(
        own,
        held(index),
        held(far),
        held(low),
        held(high),
        held(plus),
        held(minus),
        held(mult),
        held(wu),
        held(w0),
        held(w1),
        held(leaf_far),
        held(to_stress),
        held(local_own),
        held(near_part),
    )


def solution(mesh):
    return jax.shard_map(
        body,
        mesh=mesh,
        in_specs=(
            P(None, "leaf"),
            P(),
            P(),
            P(),
            P(),
            P(),
            P(),
            P(),
            P("leaf", None),
            P(None, "leaf"),
            P(None, "leaf"),
        ),
        out_specs=P(None, "leaf"),
        check_vma=False,
    )
```

profile of v0, /device:TPU:0, one launch (start us, length us, event | category | flops | bytes accessed | tf_op | source)
XLA Modules:
  0.0 54.6 jit_solution(5264372056070551594)
XLA Ops:
  0.0 5.1 %send.1 = (bf16[128,32,128]{2,1,0:T(8,128)(2,1)}, bf16[320,128]{1,0:T(8,128)(2,1)S(1)}, bf16[320,128]{1,0:T(8,128)(2,1)S(1)}, bf16[96,128]{1,0:T(8,128)(2,1)S(1)...) custom-call(s32[1]{0:T(128)} %bitcast.own, ...), custom_call_target="tpu_custom_call" | custom-call | tf_op jit(solution)/shard_map/send/pallas_call | solution.py:346
  5.1 0.0 copy-start.3
  5.1 0.0 copy-start.4
  5.1 0.0 copy-start.5
  5.1 11.2 %all-to-all-start = ((bf16[128,32,128]{2,1,0:T(8,128)(2,1)}), bf16[128,32,128]{2,1,0:T(8,128)(2,1)S(1)}, u32[]{:S(2)}, u32[]{:S(2)}) async-start(bf16[128,32,128]{2,1,0:T(8,128)(2,1)} %get-tuple-element.20), calls=%async_computation | async-start | bytes 2097152 | tf_op jit(solution)/shard_map/all_to_all | solution.py:370
  16.3 0.1 collective-permute-start
  16.4 7.2 %collective-permute-start.1 = (bf16[320,128]{1,0:T(8,128)(2,1)S(1)}, bf16[320,128]{1,0:T(8,128)(2,1)S(1)}, u32[]{:S(2)}, u32[]{:S(2)}) collective-permute-start(bf16[320,128]{1,0:T(8,128)(2,1)S(1)} %get-tuple-element.22), channel_id=1, source_target_pairs={{0,127},{1,0},{2,1},{3,2},{4,3},{5,4},{6,5},{7,6},{8,7},{9,8},{10,... | collective-permute-start | bytes 245768 | tf_op jit(solution)/shard_map/ppermute | solution.py:323
  23.5 0.0 copy-done.3
  23.5 0.0 copy-done.4
  23.5 0.0 copy-done.5
  23.6 1.5 %tree.1 = (s32[56,128]{1,0:T(8,128)S(1)}, f32[256,128]{1,0:T(8,128)S(1)}, bf16[128,768]{1,0:T(8,128)(2,1)S(1)}, bf16[128,768]{1,0:T(8,128)(2,1)S(1)}) custom-call(s32[1]{0:T(128)} %bitcast.own, s32[27,256]{1,0:T(8,128)S(1)} %copy-done.5, f32[512,128]{1,0:T(8,128)S(1)} %get-tuple-element.18.agg, f32[121,2,121]{2,1,0:T(2,128)S(1)} %bitcast.5, ...), custom_call_target="tpu_custom_call" | custom-call | flops 1000000000 | bytes 1000000 | tf_op jit(solution)/shard_map/tree/pallas_call | solution.py:378
  25.1 0.0 copy-start.2
  25.1 10.9 %collective-permute-done.low = bf16[320,128]{1,0:T(8,128)(2,1)S(1)} collective-permute-done((bf16[320,128]{1,0:T(8,128)(2,1)S(1)}, bf16[320,128]{1,0:T(8,128)(2,1)S(1)}, u32[]{:S(2)}, u32[]{:S(2)}) %collective-permute-start) | collective-permute-done | bytes 81952 | tf_op jit(solution)/shard_map/ppermute | solution.py:323
  36.0 0.0 collective-permute-done.1.high
  36.1 0.1 collective-permute-start.2
  36.1 0.0 copy-start.6
  36.2 7.7 %collective-permute-start.3 = (bf16[288,128]{1,0:T(8,128)(2,1)S(1)}, bf16[288,128]{1,0:T(8,128)(2,1)S(1)}, u32[]{:S(2)}, u32[]{:S(2)}) collective-permute-start(bf16[288,128]{1,0:T(8,128)(2,1)S(1)} %pad_maximum_fusion.1), channel_id=1, source_target_pairs={{0,125},{1,126},{2,127},{3,0},{4,1},{5,2},{6,3},{7,4},{8,5},{9,6},... | collective-permute-start | bytes 221192 | tf_op jit(solution)/shard_map/ppermute | solution.py:323
  43.9 0.0 copy-done.2
  43.9 0.0 copy-done.6
  43.9 0.0 copy-start
  43.9 0.0 copy-start.1
  43.9 1.8 %near.1.near_part = f32[128,256]{1,0:T(8,128)S(1)} custom-call(s32[1]{0:T(128)} %bitcast.own, bf16[256,128]{1,0:T(8,128)(2,1)S(1)} %get-tuple-element.30.slip_rows, bf16[320,128]{1,0:T(8,128)(2,1)S(1)} %collective-permute-done.low, bf16[320,128]{1,0:T(8,128)(2,1)S(1)} %collective-permute-done.1.high, s32[9,256]{1,0:T(8,128)S(1)} %copy-done.6, ...), custom_call_target="tpu_custom_call" | custom-call | flops 1000000000 | bytes 1000000 | tf_op jit(solution)/shard_map/near/pallas_call | solution.py:393
  45.7 0.0 collective-permute-done.2.plus
  45.7 0.1 collective-permute-done.3.minus
  45.8 0.0 all-to-all-done.far
  45.8 0.0 copy-done
  45.9 0.0 copy-done.1
  45.9 8.6 %leaf.1 = f32[128,256]{1,0:T(8,128)} custom-call(s32[1]{0:T(128)} %bitcast.own, s32[56,128]{1,0:T(8,128)S(1)} %get-tuple-element.19.index_rows, bf16[128,32,128]{2,1,0:T(8,128)(2,1)S(1)} %all-to-all-done.far, bf16[320,128]{1,0:T(8,128)(2,1)S(1)} %collective-permute-done.low, bf16[320,128]{1,0:T(8,128)(2,1)S(1)} %collective-permute-done.1.high, ...), custom_call_target="tpu_custom_call" | custom-call | tf_op jit(solution)/shard_map/leaf/pallas_call | solution.py:404
  (4 shorter events, 0.0 us)
Async XLA Ops:
  5.1 18.4 %copy-start.3 = (f32[2,121,121]{2,0,1:T(2,128)S(1)}, f32[2,121,121]{2,0,1:T(2,128)}, u32[]{:S(2)}) copy-start(f32[2,121,121]{2,0,1:T(2,128)} %param.14) | copy-start | bytes 351388
  5.1 18.4 %copy-start.4 = (f32[2,121,121]{2,0,1:T(2,128)S(1)}, f32[2,121,121]{2,0,1:T(2,128)}, u32[]{:S(2)}) copy-start(f32[2,121,121]{2,0,1:T(2,128)} %param.15) | copy-start | bytes 351388
  5.1 18.4 %copy-start.5 = (s32[27,256]{1,0:T(8,128)S(1)}, s32[27,256]{1,0:T(8,128)}, u32[]{:S(2)}) copy-start(s32[27,256]{1,0:T(8,128)} %far_list.1) | copy-start | bytes 82948
  5.1 40.7 %all-to-all-start = ((bf16[128,32,128]{2,1,0:T(8,128)(2,1)}), bf16[128,32,128]{2,1,0:T(8,128)(2,1)S(1)}, u32[]{:S(2)}, u32[]{:S(2)}) async-start(bf16[128,32,128]{2,1,0:T(8,128)(2,1)} %get-tuple-element.20), calls=%async_computation | async-start | bytes 2097152 | tf_op jit(solution)/shard_map/all_to_all | solution.py:370
  16.3 19.7 %collective-permute-start = (bf16[320,128]{1,0:T(8,128)(2,1)S(1)}, bf16[320,128]{1,0:T(8,128)(2,1)S(1)}, u32[]{:S(2)}, u32[]{:S(2)}) collective-permute-start(bf16[320,128]{1,0:T(8,128)(2,1)S(1)} %get-tuple-element.21), channel_id=1, source_target_pairs={{0,1},{1,2},{2,3},{3,4},{4,5},{5,6},{6,7},{7,8},{8,9},{9,10},{10,1... | collective-permute-start | bytes 245768 | tf_op jit(solution)/shard_map/ppermute | solution.py:323
  16.4 19.6 %collective-permute-start.1 = (bf16[320,128]{1,0:T(8,128)(2,1)S(1)}, bf16[320,128]{1,0:T(8,128)(2,1)S(1)}, u32[]{:S(2)}, u32[]{:S(2)}) collective-permute-start(bf16[320,128]{1,0:T(8,128)(2,1)S(1)} %get-tuple-element.22), channel_id=1, source_target_pairs={{0,127},{1,0},{2,1},{3,2},{4,3},{5,4},{6,5},{7,6},{8,7},{9,8},{10,... | collective-permute-start | bytes 245768 | tf_op jit(solution)/shard_map/ppermute | solution.py:323
  25.1 18.8 %copy-start.2 = (bf16[9,128,128]{2,1,0:T(8,128)(2,1)S(1)}, bf16[9,128,128]{2,1,0:T(8,128)(2,1)}, u32[]{:S(2)}) copy-start(bf16[9,128,128]{2,1,0:T(8,128)(2,1)} %blocks.1) | copy-start | bytes 884740
  36.1 9.6 %collective-permute-start.2 = (bf16[288,128]{1,0:T(8,128)(2,1)S(1)}, bf16[288,128]{1,0:T(8,128)(2,1)S(1)}, u32[]{:S(2)}, u32[]{:S(2)}) collective-permute-start(bf16[288,128]{1,0:T(8,128)(2,1)S(1)} %pad_maximum_fusion), channel_id=1, source_target_pairs={{0,3},{1,4},{2,5},{3,6},{4,7},{5,8},{6,9},{7,10},{8,11},{9,12},{10... | collective-permute-start | bytes 221192 | tf_op jit(solution)/shard_map/ppermute | solution.py:323
  36.1 7.7 %copy-start.6 = (s32[9,256]{1,0:T(8,128)S(1)}, s32[9,256]{1,0:T(8,128)}, u32[]{:S(2)}) copy-start(s32[9,256]{1,0:T(8,128)} %lists.1) | copy-start | bytes 27652
  36.2 9.7 %collective-permute-start.3 = (bf16[288,128]{1,0:T(8,128)(2,1)S(1)}, bf16[288,128]{1,0:T(8,128)(2,1)S(1)}, u32[]{:S(2)}, u32[]{:S(2)}) collective-permute-start(bf16[288,128]{1,0:T(8,128)(2,1)S(1)} %pad_maximum_fusion.1), channel_id=1, source_target_pairs={{0,125},{1,126},{2,127},{3,0},{4,1},{5,2},{6,3},{7,4},{8,5},{9,6},... | collective-permute-start | bytes 221192 | tf_op jit(solution)/shard_map/ppermute | solution.py:323
  43.9 2.0 %copy-start = (bf16[27,121,121]{2,1,0:T(8,128)(2,1)S(1)}, bf16[27,121,121]{2,1,0:T(8,128)(2,1)}, u32[]{:S(2)}) copy-start(bf16[27,121,121]{2,1,0:T(8,128)(2,1)} %leaf_far.1) | copy-start | bytes 2371846
  43.9 2.0 %copy-start.1 = (bf16[128,121]{1,0:T(8,128)(2,1)S(1)}, bf16[128,121]{1,0:T(8,128)(2,1)}, u32[]{:S(2)}) copy-start(bf16[128,121]{1,0:T(8,128)(2,1)} %to_stress.1) | copy-start | bytes 92932
where the time goes:
time: 54.9 us; the launch traced here: 54.6 us
  starting transfers between devices  26.2 us (48%)
  Pallas kernels  17.1 us (31%)
  waiting for transfers between devices  11.1 us (20%)
    ppermute x4, starting transfers between devices, shifted(): lax.ppermute(block, 'leaf', [(i, (i + by) % count) for i in range(count)])  15 us
    all_to_all x1, starting transfers between devices, body(): lax.all_to_all(far_send, 'leaf', split_axis=0, concat_axis=0, tiled=True)  11.2 us
    ppermute x4, waiting for transfers between devices, shifted(): lax.ppermute(block, 'leaf', [(i, (i + by) % count) for i in range(count)])  11.1 us
    pallas_call x1, Pallas kernels, body(): pl.pallas_call(leaf_kernel, out_shape=shape((elems, cells), F32), in_spec...  8.6 us
    pallas_call x1, Pallas kernels, body(): pl.pallas_call(send_kernel, out_shape=[kept((devices, CAP_FAR, LANES), BF...  5.11 us
    pallas_call x1, Pallas kernels, body(): pl.pallas_call(near_kernel, out_shape=kept((elems, cells), F32), in_specs...  1.82 us
    pallas_call x1, Pallas kernels, body(): pl.pallas_call(tree_kernel, out_shape=[kept((index_rows, LANES), jnp.int3...  1.53 us
  transfers between devices with their start and end apart: 5, of which 2 were waited for; matrix products, arithmetic and copies ran while one was open for 0% of the time, Pallas kernels for 6%

commit v1 on v0

--- a/solution.py
+++ b/solution.py
@@ -13,7 +13,7 @@
 CAP_FAR = 32
 EXTRA = CAP_NEAR - CAP_FAR
 LANES = 128
-TRIPLE = 3 * LANES
+PAIR = 2 * LANES
 GROUP = 8
 MIX = 100
 OFFSETS = (-1, 1, -3, -4, -2, 3, 4, 2)
@@ -66,9 +66,16 @@
 def put_split(ref, at, block, square):
     square[: block.shape[0], : block.shape[1]] = block
     high, low = halves(square[...])
-    for part, value in enumerate((high, low, high)):
-        start = at + part * LANES
-        ref[:, start : start + LANES] = value
+    ref[:, at : at + LANES] = high
+    ref[:, at + LANES : at + PAIR] = low
+
+
+def weights(ref, *starts):
+    parts = []
+    for at in starts:
+        high = ref[:, at : at + LANES]
+        parts += [high, ref[:, at + LANES : at + PAIR], high]
+    return lanes(parts)
 
 
 def bit_order(size, bits):
@@ -87,8 +94,9 @@
     ).astype(BF16)
 
 
-def send_kernel(own, slip, to_mult, up_shift, send, far_out, up_out, down_out, plus_out,
-                minus_out, mult_out, slip_out, agg_out, wu, tm, lists, square):
+def send_kernel(own, slip, to_mult, up_shift, send, far_hbm, up_out, down_out, plus_out,
+                minus_out, mult_out, slip_out, agg_out, wu, far_out, sent, tm,
+                lists, square):
     cells = slip.shape[1]
     coef = to_mult.shape[0]
     devices = send.shape[0]
@@ -97,7 +105,7 @@
     tm[:coef, :] = to_mult[...]
     square[...] = jnp.zeros_like(square)
     put_split(wu, 0, up_shift[:, 0, :], square)
-    put_split(wu, TRIPLE, up_shift[:, 1, :], square)
+    put_split(wu, PAIR, up_shift[:, 1, :], square)
     unit = one_hot(iota((cells, cells), 0), iota((cells, cells), 1))
     slip_rows = bdot(unit, slip[...], NT).astype(BF16)
     slip_out[...] = slip_rows
@@ -110,7 +118,9 @@
         agg_out[start : start + size, :] = level
         start += size
         size //= 2
-        level = bdot(lanes(tripled(level[:size]) + tripled(level[size:])), wu[...], NT)
+        level = bdot(
+            lanes(tripled(level[:size]) + tripled(level[size:])), weights(wu, 0, PAIR), NT
+        )
     spread = one_hot(iota((LANES, LANES), 0) % 4 + coef, iota((LANES, LANES), 1))
     own_row = (iota((CAP_FAR, LANES), 1) // 4) == iota((CAP_FAR, LANES), 0)
     placed = jnp.where(own_row, level, 0.0).astype(BF16)
@@ -121,6 +131,7 @@
     far_match = matches(lambda at: at < CAP_FAR, CAP_FAR, cells)
     cell_row = iota((CAP_FAR, cells), 1).astype(F32)
     turned = lists[...].T
+    copies = []
     for first in range(0, devices, GROUP):
         group = range(first, first + GROUP)
         if first // GROUP % MIX == 0:
@@ -131,6 +142,14 @@
         far_out[first : first + GROUP] = (
             (bdot(hot, mult, NN) + tail).astype(BF16).reshape(GROUP, CAP_FAR, LANES)
         )
+        copies.append(
+            pltpu.make_async_copy(
+                far_out.at[pl.ds(first, GROUP)],
+                far_hbm.at[pl.ds(first, GROUP)],
+                sent.at[first // GROUP],
+            )
+        )
+        copies[-1].start()
     lane = iota((EXTRA, LANES), 1)
     own_slot = lane == iota((EXTRA, LANES), 0) + CAP_FAR
     rest = jnp.where(lane == 0, 1.0, 0.0)
@@ -144,9 +163,12 @@
         ref[place * EXTRA : (place + 1) * EXTRA, :] = bdot(hot, mult, NN).astype(BF16)
     up_out[3 * EXTRA :, :] = slip_rows[cells - HALO :]
     down_out[3 * EXTRA :, :] = slip_rows[:HALO]
-
-
-def tree_kernel(own, far_list, agg, down_shift, sibling, index_out, local_out, w0, w1, square):
+    for copy in copies:
+        copy.wait()
+
+
+def tree_kernel(own, far_list, agg, down_shift, sibling, index_out, local_out, wd, path, ws,
+                square):
     cells = far_list.shape[1]
     kinds = far_list.shape[0]
     bits = cells.bit_length() - 1
@@ -167,24 +189,36 @@
             :, part * LANES : (part + 1) * LANES
         ]
     square[...] = jnp.zeros_like(square)
-    for ref, which in ((w0, 0), (w1, 1)):
-        put_split(ref, 0, down_shift[:, which, :], square)
-        put_split(ref, TRIPLE, sibling[:, which, :], square)
+    for which in (0, 1):
+        put_split(wd, which * PAIR, down_shift[:, which, :], square.at[which])
+        put_split(ws, which * PAIR, sibling[:, which, :], square.at[2 + which])
+    walked = None
+    for depth in range(devices.bit_length() - 1):
+        even = ((own[0] >> depth) & 1) == 0
+        down = jnp.where(even, square[0], square[1])
+        side = jnp.where(even, square[2], square[3])
+        if walked is not None:
+            high, low = halves(lanes([down, side]))
+            both = bdot(lanes(tripled(walked)), rows([high, low, high]), NN)
+            down, side = both[:, :LANES], both[:, LANES:]
+        walked = down
+        high, low = halves(side)
+        path[:, depth * PAIR : (depth + 1) * PAIR] = lanes([high, low])
     starts = [0]
     for height in range(bits):
         starts.append(starts[-1] + (cells >> height))
     local = None
     for height in reversed(range(bits)):
         parts = []
-        for which, weights in ((0, w0), (1, w1)):
+        for which in (0, 1):
             total = None
             if local is not None:
-                total = bdot(lanes(tripled(local)), weights[:, :TRIPLE], NT)
+                total = bdot(lanes(tripled(local)), weights(wd, which * PAIR), NT)
             if height >= 1:
                 half = cells >> (height + 1)
                 at = starts[height] + (1 - which) * half
                 other = bdot(
-                    lanes(tripled(agg[at : at + half, :])), weights[:, TRIPLE:], NT
+                    lanes(tripled(agg[at : at + half, :])), weights(ws, which * PAIR), NT
                 )
                 total = other if total is None else total + other
             parts.append(total)
@@ -213,17 +247,19 @@
     out[...] = total.T
 
 
-def top_levels(own, far, wu, w0, w1, levels, coef, bits, tree_bits, result):
+def top_levels(own, far, wu, wd, path, local_own, levels, coef, bits, tree_bits, result):
     devices = far.shape[0]
     spread = one_hot(iota((LANES, LANES), 0), iota((LANES, LANES), 1) % 4 + coef)
     keep = (iota((CAP_FAR, LANES), 1) // 4 == iota((CAP_FAR, LANES), 0)) & (
         iota((CAP_FAR, LANES), 1) < coef
     )
-    roots = bdot(far[...].reshape(devices * CAP_FAR, LANES), spread, NN)
-    roots = roots.reshape(devices, CAP_FAR, LANES)
-    roots = jnp.sum(jnp.where(keep[None], roots, 0.0), axis=1).astype(BF16)
-    level = bdot(bit_order(devices, tree_bits), roots, NN)
-    yield
+    found = []
+    for first in range(0, devices, 16):
+        part = bdot(far[first : first + 16].reshape(16 * CAP_FAR, LANES), spread, NN)
+        part = jnp.where(keep[None], part.reshape(16, CAP_FAR, LANES), 0.0)
+        found.append(jnp.sum(part, axis=1))
+        yield
+    level = bdot(bit_order(devices, tree_bits), rows(found).astype(BF16), NN)
     start, size = 0, devices
     starts = []
     for depth in range(tree_bits):
@@ -232,29 +268,28 @@
         start += size
         size //= 2
         if depth + 1 < tree_bits:
-            level = bdot(lanes(tripled(level[:size]) + tripled(level[size:])), wu[...], NT)
+            stacked = lanes(tripled(level[:size]) + tripled(level[size:]))
+            level = bdot(stacked, weights(wu, 0, PAIR), NT)
             yield
-    local = jnp.zeros((1, LANES), F32)
-    for depth in reversed(range(tree_bits)):
-        node = own[0] >> depth
-        place = starts[depth] + reversed_bits(node ^ 1, tree_bits - depth)
-        other = levels[pl.ds(place, 1), :]
-        stacked = lanes(tripled(local) + tripled(other))
-        first = bdot(stacked, w0[...], NT)
-        second = bdot(stacked, w1[...], NT)
-        local = jnp.where((node & 1) == 0, first, second)
+    others = []
+    for depth in range(tree_bits):
+        place = starts[depth] + reversed_bits((own[0] >> depth) ^ 1, tree_bits - depth)
+        others += tripled(levels[pl.ds(place, 1), :])
+    local = bdot(lanes(others), weights(path, *range(0, tree_bits * PAIR, PAIR)), NT)
+    yield
+    for _ in range(bits):
+        stacked = lanes(tripled(local))
+        local = rows([bdot(stacked, weights(wd, at), NT) for at in (0, PAIR)])
         yield
-    for step in range(bits):
-        stacked = lanes(tripled(local))
-        local = rows([bdot(stacked, w0[:, :TRIPLE], NT), bdot(stacked, w1[:, :TRIPLE], NT)])
-        if step + 1 == bits:
-            result.append(local)
-        yield
-
-
-def leaf_kernel(own, index_rows, far, low, high, plus, minus, mult, wu, w0, w1, leaf_far,
-                to_stress, local_own, near_part, out, index, arrived, table, levels, ts,
-                *buffers):
+    cells = 1 << bits
+    high, low = halves(local_own[...] + local)
+    order = bit_order(cells, bits)
+    result.append(bdot(order, high, NN) + bdot(order, low, NN))
+    yield
+
+
+def leaf_kernel(own, index_rows, far, low, high, plus, minus, mult, wu, wd, path,
+                leaf_far, to_stress, local_own, near_part, out, index, arrived, table, levels, ts, *buffers):
     devices = far.shape[0]
     cells = mult.shape[0]
     coef = leaf_far.shape[1]
@@ -277,21 +312,22 @@
 
     load.wait()
     result = []
-    tree = top_levels(own, far, wu, w0, w1, levels, coef, bits, tree_bits, result)
+    tree = top_levels(
+        own, far, wu, wd, path, local_own, levels, coef, bits, tree_bits, result
+    )
     count = len(buffers)
-    total = local_own[:, :coef]
+    total = jnp.zeros((cells, coef), F32)
     for kind in range(TYPES):
         buffer = buffers[kind % count]
-        for cell in range(cells):
+        for turn in range(cells):
+            cell = reversed_bits(turn, bits)
             spot = kind * cells + cell
             row = index[spot // LANES, spot % LANES]
-            spot = reversed_bits(cell, bits)
-            buffer[spot : spot + 1, :] = table[pl.ds(row, 1), :]
+            buffer[cell : cell + 1, :] = table[pl.ds(row, 1), :]
         total = total + bdot(buffer[...].astype(BF16)[:, :coef], leaf_far[kind], NT)
         next(tree, None)
     total = total + result[0][:, :coef]
-    expansion = bdot(bit_order(cells, bits), total.astype(BF16), NN).astype(BF16)
-    out[...] = bdot(ts[:, :coef], expansion, NT) + near_part[...]
+    out[...] = bdot(ts[:, :coef], total.astype(BF16), NT) + near_part[...]
 
 
 def shape(dims, dtype):
@@ -304,6 +340,10 @@
 
 def held(x):
     return pltpu.with_memory_space_constraint(x, pltpu.VMEM)
+
+
+def outer(x):
+    return pltpu.with_memory_space_constraint(x, pltpu.HBM)
 
 
 def limits(mib):
@@ -346,7 +386,7 @@
     far_send, up_send, down_send, plus_own, minus_own, mult, slip_rows, agg, wu = pl.pallas_call(
         send_kernel,
         out_shape=[
-            kept((devices, CAP_FAR, LANES), BF16),
+            shape((devices, CAP_FAR, LANES), BF16),
             kept((bundle, LANES), BF16),
             kept((bundle, LANES), BF16),
             kept((EXTRA, LANES), BF16),
@@ -354,38 +394,45 @@
             kept((cells, LANES), BF16),
             kept((cells, elems), BF16),
             kept((2 * cells, LANES), F32),
-            kept((LANES, 2 * TRIPLE), BF16),
+            kept((LANES, 2 * PAIR), BF16),
         ],
         in_specs=[SM, VM, VM, VM, VM],
-        out_specs=[VM] * 9,
+        out_specs=[pl.BlockSpec(memory_space=pl.ANY)] + [VM] * 8,
         scratch_shapes=[
+            scratch((devices, CAP_FAR, LANES), BF16),
+            pltpu.SemaphoreType.DMA((devices // GROUP,)),
             scratch((LANES, elems), BF16),
             scratch((devices, CAP_NEAR), F32),
             scratch((LANES, LANES), F32),
         ],
+        compiler_params=limits(16),
         name="send",
-    )(own, slip, to_multipole, up_t, send_cells.reshape(devices, CAP_NEAR))
+    )(
+        own,
+        *(outer(x) for x in (slip, to_multipole, up_t, send_cells.reshape(devices, CAP_NEAR))),
+    )
     low = shifted(up_send, 1)
     high = shifted(down_send, -1)
     far = lax.all_to_all(far_send, "leaf", split_axis=0, concat_axis=0, tiled=True)
-    plus = shifted(
-        rows([plus_own, low[EXTRA : 2 * EXTRA], high[2 * EXTRA : 3 * EXTRA]]), 3
-    )
+    plus = shifted(rows([plus_own, low[EXTRA : 2 * EXTRA], high[2 * EXTRA : 3 * EXTRA]]), 3)
     minus = shifted(
         rows([minus_own, high[EXTRA : 2 * EXTRA], low[2 * EXTRA : 3 * EXTRA]]), -3
     )
     index_rows = (TYPES * cells // LANES + 7) // 8 * 8
-    index, local_own, w0, w1 = pl.pallas_call(
+    index, local_own, wd, path = pl.pallas_call(
         tree_kernel,
         out_shape=[
             kept((index_rows, LANES), jnp.int32),
             kept((cells, LANES), F32),
-            kept((LANES, 2 * TRIPLE), BF16),
-            kept((LANES, 2 * TRIPLE), BF16),
+            kept((LANES, 2 * PAIR), BF16),
+            kept((LANES, (devices.bit_length() - 1) * PAIR), BF16),
         ],
         in_specs=[SM, VM, VM, VM, VM],
         out_specs=[VM] * 4,
-        scratch_shapes=[scratch((LANES, LANES), F32)],
+        scratch_shapes=[
+            scratch((LANES, 2 * PAIR), BF16),
+            scratch((4, LANES, LANES), F32),
+        ],
         cost_estimate=cost(10**9),
         compiler_params=limits(16),
         name="tree",
@@ -395,7 +442,10 @@
         out_shape=kept((elems, cells), F32),
         in_specs=[SM] + [VM] * 5,
         out_specs=VM,
-        scratch_shapes=[scratch((TRIPLE, elems), BF16), scratch((LANES, cells), F32)],
+        scratch_shapes=[
+            scratch((cells + LANES, elems), BF16),
+            scratch((LANES, cells), F32),
+        ],
         cost_estimate=cost(10**9),
         compiler_params=limits(16),
         name="near",
@@ -404,7 +454,7 @@
     return pl.pallas_call(
         leaf_kernel,
         out_shape=shape((elems, cells), F32),
-        in_specs=[SM] + [VM] * 14,
+        in_specs=[SM] + [VM] * 10 + [VM] * 4,
         out_specs=VM,
         scratch_shapes=[
             pltpu.SMEM((index_rows, LANES), jnp.int32),
@@ -426,8 +476,8 @@
         held(minus),
         held(mult),
         held(wu),
-        held(w0),
-        held(w1),
+        held(wd),
+        held(path),
         held(leaf_far),
         held(to_stress),
         held(local_own),

time: 54.9 us -> 54.6 us (level)
  waiting for transfers between devices: 11.1 us -> 10.2 us
    pallas_call x1, Pallas kernels: 1.53 us -> 2.35 us  [body(): pl.pallas_call(tree_kernel, out_shape=[kept((index_rows, LANES), jnp.int3...]
    ppermute x4, waiting for transfers between devices: 11.1 us -> 10.2 us  [shifted(): lax.ppermute(block, 'leaf', [(i, (i + by) % count) for i in range(count)])]
  transfers between devices with their start and end apart: 5 -> 5, of which waited for: 2 -> 2; matrix products, arithmetic and copies ran while one was open for 0% -> 0% of each run, Pallas kernels for 6% -> 8%
where the time goes in v1:
time: 54.6 us; the launch traced here: 54.3 us
  starting transfers between devices  26.2 us (48%)
  Pallas kernels  17.5 us (32%)
  waiting for transfers between devices  10.2 us (19%)
    ppermute x4, starting transfers between devices, shifted(): lax.ppermute(block, 'leaf', [(i, (i + by) % count) for i in range(count)])  15 us
    all_to_all x1, starting transfers between devices, body(): lax.all_to_all(far_send, 'leaf', split_axis=0, concat_axis=0, tiled=True)  11.2 us
    ppermute x4, waiting for transfers between devices, shifted(): lax.ppermute(block, 'leaf', [(i, (i + by) % count) for i in range(count)])  10.2 us
    pallas_call x1, Pallas kernels, body(): pl.pallas_call(leaf_kernel, out_shape=shape((elems, cells), F32), in_spec...  8.47 us
    pallas_call x1, Pallas kernels, body(): pl.pallas_call(send_kernel, out_shape=[shape((devices, CAP_FAR, LANES), B...  4.91 us
    pallas_call x1, Pallas kernels, body(): pl.pallas_call(tree_kernel, out_shape=[kept((index_rows, LANES), jnp.int3...  2.35 us
    pallas_call x1, Pallas kernels, body(): pl.pallas_call(near_kernel, out_shape=kept((elems, cells), F32), in_specs...  1.82 us
  transfers between devices with their start and end apart: 5, of which 2 were waited for; matrix products, arithmetic and copies ran while one was open for 0% of the time, Pallas kernels for 8%

profile of v1, /device:TPU:0, one launch (start us, length us, event | category | flops | bytes accessed | tf_op | source)
XLA Modules:
  0.0 54.3 jit_solution(16528279310190058530)
XLA Ops:
  0.0 4.9 %send.1 = (bf16[128,32,128]{2,1,0:T(8,128)(2,1)}, bf16[320,128]{1,0:T(8,128)(2,1)S(1)}, bf16[320,128]{1,0:T(8,128)(2,1)S(1)}, bf16[96,128]{1,0:T(8,128)(2,1)S(1)...) custom-call(s32[1]{0:T(128)} %bitcast.own, ...), custom_call_target="tpu_custom_call" | custom-call | tf_op jit(solution)/shard_map/send/pallas_call | solution.py:386
  4.9 0.0 copy-start.3
  4.9 0.0 copy-start.4
  4.9 0.0 copy-start.5
  5.0 11.2 %all-to-all-start = ((bf16[128,32,128]{2,1,0:T(8,128)(2,1)}), bf16[128,32,128]{2,1,0:T(8,128)(2,1)S(1)}, u32[]{:S(2)}, u32[]{:S(2)}) async-start(bf16[128,32,128]{2,1,0:T(8,128)(2,1)} %get-tuple-element.20), calls=%async_computation | async-start | bytes 2097152 | tf_op jit(solution)/shard_map/all_to_all | solution.py:416
  16.1 0.1 collective-permute-start
  16.2 7.2 %collective-permute-start.1 = (bf16[320,128]{1,0:T(8,128)(2,1)S(1)}, bf16[320,128]{1,0:T(8,128)(2,1)S(1)}, u32[]{:S(2)}, u32[]{:S(2)}) collective-permute-start(bf16[320,128]{1,0:T(8,128)(2,1)S(1)} %get-tuple-element.22), channel_id=1, source_target_pairs={{0,127},{1,0},{2,1},{3,2},{4,3},{5,4},{6,5},{7,6},{8,7},{9,8},{10,... | collective-permute-start | bytes 245768 | tf_op jit(solution)/shard_map/ppermute | solution.py:363
  23.4 0.0 copy-done.3
  23.4 0.0 copy-done.4
  23.4 0.0 copy-done.5
  23.4 2.4 %tree.1 = (s32[56,128]{1,0:T(8,128)S(1)}, f32[256,128]{1,0:T(8,128)S(1)}, bf16[128,512]{1,0:T(8,128)(2,1)S(1)}, bf16[128,1792]{1,0:T(8,128)(2,1)S(1)}) custom-call(s32[1]{0:T(128)} %bitcast.own, s32[27,256]{1,0:T(8,128)S(1)} %copy-done.5, f32[512,128]{1,0:T(8,128)S(1)} %get-tuple-element.18.agg, f32[121,2,121]{2,1,0:T(2,128)S(1)} %bitcast.5, ...), custom_call_target="tpu_custom_call" | custom-call | flops 1000000000 | bytes 1000000 | tf_op jit(solution)/shard_map/tree/pallas_call | solution.py:422
  25.7 0.0 copy-start.2
  25.8 10.1 %collective-permute-done.low = bf16[320,128]{1,0:T(8,128)(2,1)S(1)} collective-permute-done((bf16[320,128]{1,0:T(8,128)(2,1)S(1)}, bf16[320,128]{1,0:T(8,128)(2,1)S(1)}, u32[]{:S(2)}, u32[]{:S(2)}) %collective-permute-start) | collective-permute-done | bytes 81952 | tf_op jit(solution)/shard_map/ppermute | solution.py:363
  35.9 0.0 collective-permute-done.1.high
  35.9 0.1 collective-permute-start.2
  36.0 0.0 copy-start.6
  36.0 7.7 %collective-permute-start.3 = (bf16[288,128]{1,0:T(8,128)(2,1)S(1)}, bf16[288,128]{1,0:T(8,128)(2,1)S(1)}, u32[]{:S(2)}, u32[]{:S(2)}) collective-permute-start(bf16[288,128]{1,0:T(8,128)(2,1)S(1)} %pad_maximum_fusion.1), channel_id=1, source_target_pairs={{0,125},{1,126},{2,127},{3,0},{4,1},{5,2},{6,3},{7,4},{8,5},{9,6},... | collective-permute-start | bytes 221192 | tf_op jit(solution)/shard_map/ppermute | solution.py:363
  43.7 0.0 copy-done.2
  43.7 0.0 copy-done.6
  43.7 0.0 copy-start
  43.7 0.0 copy-start.1
  43.7 1.8 %near.1.near_part = f32[128,256]{1,0:T(8,128)S(1)} custom-call(s32[1]{0:T(128)} %bitcast.own, bf16[256,128]{1,0:T(8,128)(2,1)S(1)} %get-tuple-element.30.slip_rows, bf16[320,128]{1,0:T(8,128)(2,1)S(1)} %collective-permute-done.low, bf16[320,128]{1,0:T(8,128)(2,1)S(1)} %collective-permute-done.1.high, s32[9,256]{1,0:T(8,128)S(1)} %copy-done.6, ...), custom_call_target="tpu_custom_call" | custom-call | flops 1000000000 | bytes 1000000 | tf_op jit(solution)/shard_map/near/pallas_call | solution.py:440
  45.5 0.0 collective-permute-done.2.plus
  45.6 0.1 collective-permute-done.3.minus
  45.7 0.0 all-to-all-done.far
  45.7 0.0 copy-done
  45.7 0.0 copy-done.1
  45.7 8.5 %leaf.1 = f32[128,256]{1,0:T(8,128)} custom-call(s32[1]{0:T(128)} %bitcast.own, s32[56,128]{1,0:T(8,128)S(1)} %get-tuple-element.19.index_rows, bf16[128,32,128]{2,1,0:T(8,128)(2,1)S(1)} %all-to-all-done.far, bf16[320,128]{1,0:T(8,128)(2,1)S(1)} %collective-permute-done.low, bf16[320,128]{1,0:T(8,128)(2,1)S(1)} %collective-permute-done.1.high, ...), custom_call_target="tpu_custom_call" | custom-call | tf_op jit(solution)/shard_map/leaf/pallas_call | solution.py:454
  (4 shorter events, 0.0 us)
Async XLA Ops:
  4.9 18.5 %copy-start.3 = (f32[2,121,121]{2,0,1:T(2,128)S(1)}, f32[2,121,121]{2,0,1:T(2,128)}, u32[]{:S(2)}) copy-start(f32[2,121,121]{2,0,1:T(2,128)} %param.14) | copy-start | bytes 351388
  4.9 18.5 %copy-start.4 = (f32[2,121,121]{2,0,1:T(2,128)S(1)}, f32[2,121,121]{2,0,1:T(2,128)}, u32[]{:S(2)}) copy-start(f32[2,121,121]{2,0,1:T(2,128)} %param.15) | copy-start | bytes 351388
  4.9 18.4 %copy-start.5 = (s32[27,256]{1,0:T(8,128)S(1)}, s32[27,256]{1,0:T(8,128)}, u32[]{:S(2)}) copy-start(s32[27,256]{1,0:T(8,128)} %far_list.1) | copy-start | bytes 82948
  5.0 40.7 %all-to-all-start = ((bf16[128,32,128]{2,1,0:T(8,128)(2,1)}), bf16[128,32,128]{2,1,0:T(8,128)(2,1)S(1)}, u32[]{:S(2)}, u32[]{:S(2)}) async-start(bf16[128,32,128]{2,1,0:T(8,128)(2,1)} %get-tuple-element.20), calls=%async_computation | async-start | bytes 2097152 | tf_op jit(solution)/shard_map/all_to_all | solution.py:416
  16.1 19.7 %collective-permute-start = (bf16[320,128]{1,0:T(8,128)(2,1)S(1)}, bf16[320,128]{1,0:T(8,128)(2,1)S(1)}, u32[]{:S(2)}, u32[]{:S(2)}) collective-permute-start(bf16[320,128]{1,0:T(8,128)(2,1)S(1)} %get-tuple-element.21), channel_id=1, source_target_pairs={{0,1},{1,2},{2,3},{3,4},{4,5},{5,6},{6,7},{7,8},{8,9},{9,10},{10,1... | collective-permute-start | bytes 245768 | tf_op jit(solution)/shard_map/ppermute | solution.py:363
  16.2 19.6 %collective-permute-start.1 = (bf16[320,128]{1,0:T(8,128)(2,1)S(1)}, bf16[320,128]{1,0:T(8,128)(2,1)S(1)}, u32[]{:S(2)}, u32[]{:S(2)}) collective-permute-start(bf16[320,128]{1,0:T(8,128)(2,1)S(1)} %get-tuple-element.22), channel_id=1, source_target_pairs={{0,127},{1,0},{2,1},{3,2},{4,3},{5,4},{6,5},{7,6},{8,7},{9,8},{10,... | collective-permute-start | bytes 245768 | tf_op jit(solution)/shard_map/ppermute | solution.py:363
  25.7 18.0 %copy-start.2 = (bf16[9,128,128]{2,1,0:T(8,128)(2,1)S(1)}, bf16[9,128,128]{2,1,0:T(8,128)(2,1)}, u32[]{:S(2)}) copy-start(bf16[9,128,128]{2,1,0:T(8,128)(2,1)} %blocks.1) | copy-start | bytes 884740
  35.9 9.6 %collective-permute-start.2 = (bf16[288,128]{1,0:T(8,128)(2,1)S(1)}, bf16[288,128]{1,0:T(8,128)(2,1)S(1)}, u32[]{:S(2)}, u32[]{:S(2)}) collective-permute-start(bf16[288,128]{1,0:T(8,128)(2,1)S(1)} %pad_maximum_fusion), channel_id=1, source_target_pairs={{0,3},{1,4},{2,5},{3,6},{4,7},{5,8},{6,9},{7,10},{8,11},{9,12},{10... | collective-permute-start | bytes 221192 | tf_op jit(solution)/shard_map/ppermute | solution.py:363
  36.0 7.7 %copy-start.6 = (s32[9,256]{1,0:T(8,128)S(1)}, s32[9,256]{1,0:T(8,128)}, u32[]{:S(2)}) copy-start(s32[9,256]{1,0:T(8,128)} %lists.1) | copy-start | bytes 27652
  36.0 9.7 %collective-permute-start.3 = (bf16[288,128]{1,0:T(8,128)(2,1)S(1)}, bf16[288,128]{1,0:T(8,128)(2,1)S(1)}, u32[]{:S(2)}, u32[]{:S(2)}) collective-permute-start(bf16[288,128]{1,0:T(8,128)(2,1)S(1)} %pad_maximum_fusion.1), channel_id=1, source_target_pairs={{0,125},{1,126},{2,127},{3,0},{4,1},{5,2},{6,3},{7,4},{8,5},{9,6},... | collective-permute-start | bytes 221192 | tf_op jit(solution)/shard_map/ppermute | solution.py:363
  43.7 2.0 %copy-start = (bf16[27,121,121]{2,1,0:T(8,128)(2,1)S(1)}, bf16[27,121,121]{2,1,0:T(8,128)(2,1)}, u32[]{:S(2)}) copy-start(bf16[27,121,121]{2,1,0:T(8,128)(2,1)} %leaf_far.1) | copy-start | bytes 2371846
  43.7 2.0 %copy-start.1 = (bf16[128,121]{1,0:T(8,128)(2,1)S(1)}, bf16[128,121]{1,0:T(8,128)(2,1)}, u32[]{:S(2)}) copy-start(bf16[128,121]{1,0:T(8,128)(2,1)} %to_stress.1) | copy-start | bytes 92932

commit v2 on v1

--- a/solution.py
+++ b/solution.py
@@ -16,6 +16,7 @@
 PAIR = 2 * LANES
 GROUP = 8
 MIX = 100
+SLACK = 8
 OFFSETS = (-1, 1, -3, -4, -2, 3, 4, 2)
 
 VM = pl.BlockSpec(memory_space=pltpu.VMEM)
@@ -111,7 +112,7 @@
     slip_out[...] = slip_rows
     mult = bdot(slip_rows, tm[...], NT).astype(BF16)
     mult_out[...] = mult
-    lists[...] = send[...].astype(F32)
+    lists[:devices, :] = send[...].astype(F32)
     level = bdot(bit_order(cells, bits), mult, NN)
     start, size = 0, cells
     for _ in range(bits):
@@ -130,7 +131,7 @@
     rest = jnp.where(lane == CAP_FAR, 1.0, 0.0)
     far_match = matches(lambda at: at < CAP_FAR, CAP_FAR, cells)
     cell_row = iota((CAP_FAR, cells), 1).astype(F32)
-    turned = lists[...].T
+    turned = lists[:devices, :].T
     copies = []
     for first in range(0, devices, GROUP):
         group = range(first, first + GROUP)
@@ -324,7 +325,7 @@
             spot = kind * cells + cell
             row = index[spot // LANES, spot % LANES]
             buffer[cell : cell + 1, :] = table[pl.ds(row, 1), :]
-        total = total + bdot(buffer[...].astype(BF16)[:, :coef], leaf_far[kind], NT)
+        total = total + bdot(buffer[:cells, :].astype(BF16)[:, :coef], leaf_far[kind], NT)
         next(tree, None)
     total = total + result[0][:, :coef]
     out[...] = bdot(ts[:, :coef], total.astype(BF16), NT) + near_part[...]
@@ -393,7 +394,7 @@
             kept((EXTRA, LANES), BF16),
             kept((cells, LANES), BF16),
             kept((cells, elems), BF16),
-            kept((2 * cells, LANES), F32),
+            kept((2 * cells + SLACK, LANES), F32),
             kept((LANES, 2 * PAIR), BF16),
         ],
         in_specs=[SM, VM, VM, VM, VM],
@@ -402,7 +403,7 @@
             scratch((devices, CAP_FAR, LANES), BF16),
             pltpu.SemaphoreType.DMA((devices // GROUP,)),
             scratch((LANES, elems), BF16),
-            scratch((devices, CAP_NEAR), F32),
+            scratch((devices + SLACK, CAP_NEAR), F32),
             scratch((LANES, LANES), F32),
         ],
         compiler_params=limits(16),
@@ -418,7 +419,7 @@
     minus = shifted(
         rows([minus_own, high[EXTRA : 2 * EXTRA], low[2 * EXTRA : 3 * EXTRA]]), -3
     )
-    index_rows = (TYPES * cells // LANES + 7) // 8 * 8
+    index_rows = cells // LANES * ((TYPES + 7) // 8 * 8)
     index, local_own, wd, path = pl.pallas_call(
         tree_kernel,
         out_shape=[
@@ -459,11 +460,11 @@
         scratch_shapes=[
             pltpu.SMEM((index_rows, LANES), jnp.int32),
             pltpu.SemaphoreType.DMA,
-            scratch((table_rows, LANES), F32),
-            scratch((2 * devices, LANES), F32),
+            scratch((table_rows + SLACK, LANES), F32),
+            scratch((2 * devices + SLACK, LANES), F32),
             scratch((elems, LANES), BF16),
         ]
-        + [scratch((cells, LANES), F32)] * 6,
+        + [scratch((cells + SLACK, LANES), F32)] * 6,
         compiler_params=limits(24),
         name="leaf",
     )(

time: 54.6 us -> 54.7 us (level)
  no operation moved by 1% of the time
where the time goes in v2:
time: 54.7 us; the launch traced here: 54.4 us
  starting transfers between devices  26.2 us (48%)
  Pallas kernels  17.6 us (32%)
  waiting for transfers between devices  10.2 us (19%)
    ppermute x4, starting transfers between devices, shifted(): lax.ppermute(block, 'leaf', [(i, (i + by) % count) for i in range(count)])  15 us
    all_to_all x1, starting transfers between devices, body(): lax.all_to_all(far_send, 'leaf', split_axis=0, concat_axis=0, tiled=True)  11.2 us
    ppermute x4, waiting for transfers between devices, shifted(): lax.ppermute(block, 'leaf', [(i, (i + by) % count) for i in range(count)])  10.2 us
    pallas_call x1, Pallas kernels, body(): pl.pallas_call(leaf_kernel, out_shape=shape((elems, cells), F32), in_spec...  8.55 us
    pallas_call x1, Pallas kernels, body(): pl.pallas_call(send_kernel, out_shape=[shape((devices, CAP_FAR, LANES), B...  4.91 us
    pallas_call x1, Pallas kernels, body(): pl.pallas_call(tree_kernel, out_shape=[kept((index_rows, LANES), jnp.int3...  2.35 us
    pallas_call x1, Pallas kernels, body(): pl.pallas_call(near_kernel, out_shape=kept((elems, cells), F32), in_specs...  1.82 us
  transfers between devices with their start and end apart: 5, of which 2 were waited for; matrix products, arithmetic and copies ran while one was open for 0% of the time, Pallas kernels for 8%

profile of v2, /device:TPU:0, one launch (start us, length us, event | category | flops | bytes accessed | tf_op | source)
XLA Modules:
  0.0 54.4 jit_solution(1580902909017687304)
XLA Ops:
  0.0 4.9 %send.1 = (bf16[128,32,128]{2,1,0:T(8,128)(2,1)}, bf16[320,128]{1,0:T(8,128)(2,1)S(1)}, bf16[320,128]{1,0:T(8,128)(2,1)S(1)}, bf16[96,128]{1,0:T(8,128)(2,1)S(1)...) custom-call(s32[1]{0:T(128)} %bitcast.own, ...), custom_call_target="tpu_custom_call" | custom-call | tf_op jit(solution)/shard_map/send/pallas_call | solution.py:387
  4.9 0.0 copy-start.3
  4.9 0.0 copy-start.4
  4.9 0.0 copy-start.5
  5.0 11.2 %all-to-all-start = ((bf16[128,32,128]{2,1,0:T(8,128)(2,1)}), bf16[128,32,128]{2,1,0:T(8,128)(2,1)S(1)}, u32[]{:S(2)}, u32[]{:S(2)}) async-start(bf16[128,32,128]{2,1,0:T(8,128)(2,1)} %get-tuple-element.20), calls=%async_computation | async-start | bytes 2097152 | tf_op jit(solution)/shard_map/all_to_all | solution.py:417
  16.1 0.1 collective-permute-start
  16.2 7.2 %collective-permute-start.1 = (bf16[320,128]{1,0:T(8,128)(2,1)S(1)}, bf16[320,128]{1,0:T(8,128)(2,1)S(1)}, u32[]{:S(2)}, u32[]{:S(2)}) collective-permute-start(bf16[320,128]{1,0:T(8,128)(2,1)S(1)} %get-tuple-element.22), channel_id=1, source_target_pairs={{0,127},{1,0},{2,1},{3,2},{4,3},{5,4},{6,5},{7,6},{8,7},{9,8},{10,... | collective-permute-start | bytes 245768 | tf_op jit(solution)/shard_map/ppermute | solution.py:364
  23.4 0.0 copy-done.3
  23.4 0.0 copy-done.4
  23.4 0.0 copy-done.5
  23.4 2.4 %tree.1 = (s32[64,128]{1,0:T(8,128)S(1)}, f32[256,128]{1,0:T(8,128)S(1)}, bf16[128,512]{1,0:T(8,128)(2,1)S(1)}, bf16[128,1792]{1,0:T(8,128)(2,1)S(1)}) custom-call(s32[1]{0:T(128)} %bitcast.own, s32[27,256]{1,0:T(8,128)S(1)} %copy-done.5, f32[520,128]{1,0:T(8,128)S(1)} %get-tuple-element.18.agg, f32[121,2,121]{2,1,0:T(2,128)S(1)} %bitcast.5, ...), custom_call_target="tpu_custom_call" | custom-call | flops 1000000000 | bytes 1000000 | tf_op jit(solution)/shard_map/tree/pallas_call | solution.py:423
  25.7 0.0 copy-start.2
  25.8 10.1 %collective-permute-done.low = bf16[320,128]{1,0:T(8,128)(2,1)S(1)} collective-permute-done((bf16[320,128]{1,0:T(8,128)(2,1)S(1)}, bf16[320,128]{1,0:T(8,128)(2,1)S(1)}, u32[]{:S(2)}, u32[]{:S(2)}) %collective-permute-start) | collective-permute-done | bytes 81952 | tf_op jit(solution)/shard_map/ppermute | solution.py:364
  35.9 0.0 collective-permute-done.1.high
  35.9 0.1 collective-permute-start.2
  36.0 0.0 copy-start.6
  36.0 7.7 %collective-permute-start.3 = (bf16[288,128]{1,0:T(8,128)(2,1)S(1)}, bf16[288,128]{1,0:T(8,128)(2,1)S(1)}, u32[]{:S(2)}, u32[]{:S(2)}) collective-permute-start(bf16[288,128]{1,0:T(8,128)(2,1)S(1)} %pad_maximum_fusion.1), channel_id=1, source_target_pairs={{0,125},{1,126},{2,127},{3,0},{4,1},{5,2},{6,3},{7,4},{8,5},{9,6},... | collective-permute-start | bytes 221192 | tf_op jit(solution)/shard_map/ppermute | solution.py:364
  43.7 0.0 copy-done.2
  43.7 0.0 copy-done.6
  43.7 0.0 copy-start
  43.7 0.0 copy-start.1
  43.7 1.8 %near.1.near_part = f32[128,256]{1,0:T(8,128)S(1)} custom-call(s32[1]{0:T(128)} %bitcast.own, bf16[256,128]{1,0:T(8,128)(2,1)S(1)} %get-tuple-element.30.slip_rows, bf16[320,128]{1,0:T(8,128)(2,1)S(1)} %collective-permute-done.low, bf16[320,128]{1,0:T(8,128)(2,1)S(1)} %collective-permute-done.1.high, s32[9,256]{1,0:T(8,128)S(1)} %copy-done.6, ...), custom_call_target="tpu_custom_call" | custom-call | flops 1000000000 | bytes 1000000 | tf_op jit(solution)/shard_map/near/pallas_call | solution.py:441
  45.5 0.0 collective-permute-done.2.plus
  45.6 0.1 collective-permute-done.3.minus
  45.7 0.0 all-to-all-done.far
  45.7 0.0 copy-done
  45.7 0.0 copy-done.1
  45.7 8.6 %leaf.1 = f32[128,256]{1,0:T(8,128)} custom-call(s32[1]{0:T(128)} %bitcast.own, s32[64,128]{1,0:T(8,128)S(1)} %get-tuple-element.19.index_rows, bf16[128,32,128]{2,1,0:T(8,128)(2,1)S(1)} %all-to-all-done.far, bf16[320,128]{1,0:T(8,128)(2,1)S(1)} %collective-permute-done.low, bf16[320,128]{1,0:T(8,128)(2,1)S(1)} %collective-permute-done.1.high, ...), custom_call_target="tpu_custom_call" | custom-call | tf_op jit(solution)/shard_map/leaf/pallas_call | solution.py:455
  (4 shorter events, 0.0 us)
Async XLA Ops:
  4.9 18.5 %copy-start.3 = (f32[2,121,121]{2,0,1:T(2,128)S(1)}, f32[2,121,121]{2,0,1:T(2,128)}, u32[]{:S(2)}) copy-start(f32[2,121,121]{2,0,1:T(2,128)} %param.14) | copy-start | bytes 351388
  4.9 18.5 %copy-start.4 = (f32[2,121,121]{2,0,1:T(2,128)S(1)}, f32[2,121,121]{2,0,1:T(2,128)}, u32[]{:S(2)}) copy-start(f32[2,121,121]{2,0,1:T(2,128)} %param.15) | copy-start | bytes 351388
  4.9 18.4 %copy-start.5 = (s32[27,256]{1,0:T(8,128)S(1)}, s32[27,256]{1,0:T(8,128)}, u32[]{:S(2)}) copy-start(s32[27,256]{1,0:T(8,128)} %far_list.1) | copy-start | bytes 82948
  5.0 40.7 %all-to-all-start = ((bf16[128,32,128]{2,1,0:T(8,128)(2,1)}), bf16[128,32,128]{2,1,0:T(8,128)(2,1)S(1)}, u32[]{:S(2)}, u32[]{:S(2)}) async-start(bf16[128,32,128]{2,1,0:T(8,128)(2,1)} %get-tuple-element.20), calls=%async_computation | async-start | bytes 2097152 | tf_op jit(solution)/shard_map/all_to_all | solution.py:417
  16.1 19.7 %collective-permute-start = (bf16[320,128]{1,0:T(8,128)(2,1)S(1)}, bf16[320,128]{1,0:T(8,128)(2,1)S(1)}, u32[]{:S(2)}, u32[]{:S(2)}) collective-permute-start(bf16[320,128]{1,0:T(8,128)(2,1)S(1)} %get-tuple-element.21), channel_id=1, source_target_pairs={{0,1},{1,2},{2,3},{3,4},{4,5},{5,6},{6,7},{7,8},{8,9},{9,10},{10,1... | collective-permute-start | bytes 245768 | tf_op jit(solution)/shard_map/ppermute | solution.py:364
  16.2 19.6 %collective-permute-start.1 = (bf16[320,128]{1,0:T(8,128)(2,1)S(1)}, bf16[320,128]{1,0:T(8,128)(2,1)S(1)}, u32[]{:S(2)}, u32[]{:S(2)}) collective-permute-start(bf16[320,128]{1,0:T(8,128)(2,1)S(1)} %get-tuple-element.22), channel_id=1, source_target_pairs={{0,127},{1,0},{2,1},{3,2},{4,3},{5,4},{6,5},{7,6},{8,7},{9,8},{10,... | collective-permute-start | bytes 245768 | tf_op jit(solution)/shard_map/ppermute | solution.py:364
  25.7 18.0 %copy-start.2 = (bf16[9,128,128]{2,1,0:T(8,128)(2,1)S(1)}, bf16[9,128,128]{2,1,0:T(8,128)(2,1)}, u32[]{:S(2)}) copy-start(bf16[9,128,128]{2,1,0:T(8,128)(2,1)} %blocks.1) | copy-start | bytes 884740
  35.9 9.6 %collective-permute-start.2 = (bf16[288,128]{1,0:T(8,128)(2,1)S(1)}, bf16[288,128]{1,0:T(8,128)(2,1)S(1)}, u32[]{:S(2)}, u32[]{:S(2)}) collective-permute-start(bf16[288,128]{1,0:T(8,128)(2,1)S(1)} %pad_maximum_fusion), channel_id=1, source_target_pairs={{0,3},{1,4},{2,5},{3,6},{4,7},{5,8},{6,9},{7,10},{8,11},{9,12},{10... | collective-permute-start | bytes 221192 | tf_op jit(solution)/shard_map/ppermute | solution.py:364
  36.0 7.7 %copy-start.6 = (s32[9,256]{1,0:T(8,128)S(1)}, s32[9,256]{1,0:T(8,128)}, u32[]{:S(2)}) copy-start(s32[9,256]{1,0:T(8,128)} %lists.1) | copy-start | bytes 27652
  36.0 9.7 %collective-permute-start.3 = (bf16[288,128]{1,0:T(8,128)(2,1)S(1)}, bf16[288,128]{1,0:T(8,128)(2,1)S(1)}, u32[]{:S(2)}, u32[]{:S(2)}) collective-permute-start(bf16[288,128]{1,0:T(8,128)(2,1)S(1)} %pad_maximum_fusion.1), channel_id=1, source_target_pairs={{0,125},{1,126},{2,127},{3,0},{4,1},{5,2},{6,3},{7,4},{8,5},{9,6},... | collective-permute-start | bytes 221192 | tf_op jit(solution)/shard_map/ppermute | solution.py:364
  43.7 2.0 %copy-start = (bf16[27,121,121]{2,1,0:T(8,128)(2,1)S(1)}, bf16[27,121,121]{2,1,0:T(8,128)(2,1)}, u32[]{:S(2)}) copy-start(bf16[27,121,121]{2,1,0:T(8,128)(2,1)} %leaf_far.1) | copy-start | bytes 2371846
  43.7 2.0 %copy-start.1 = (bf16[128,121]{1,0:T(8,128)(2,1)S(1)}, bf16[128,121]{1,0:T(8,128)(2,1)}, u32[]{:S(2)}) copy-start(bf16[128,121]{1,0:T(8,128)(2,1)} %to_stress.1) | copy-start | bytes 92932

commit v3 on v1

--- a/solution.py
+++ b/solution.py
@@ -15,7 +15,6 @@
 LANES = 128
 PAIR = 2 * LANES
 GROUP = 8
-MIX = 100
 OFFSETS = (-1, 1, -3, -4, -2, 3, 4, 2)
 
 VM = pl.BlockSpec(memory_space=pltpu.VMEM)
@@ -129,16 +128,11 @@
     own_slot = lane == iota((CAP_FAR, LANES), 0)
     rest = jnp.where(lane == CAP_FAR, 1.0, 0.0)
     far_match = matches(lambda at: at < CAP_FAR, CAP_FAR, cells)
-    cell_row = iota((CAP_FAR, cells), 1).astype(F32)
-    turned = lists[...].T
     copies = []
     for first in range(0, devices, GROUP):
         group = range(first, first + GROUP)
-        if first // GROUP % MIX == 0:
-            hot = rows([one_hot(turned[:CAP_FAR, d : d + 1], cell_row) for d in group])
-        else:
-            spots = rows([jnp.where(own_slot, lists[d : d + 1, :], rest) for d in group])
-            hot = one_hot(bdot(spots.astype(BF16), far_match, NN), 0.0)
+        spots = rows([jnp.where(own_slot, lists[d : d + 1, :], rest) for d in group])
+        hot = one_hot(bdot(spots.astype(BF16), far_match, NN), 0.0)
         far_out[first : first + GROUP] = (
             (bdot(hot, mult, NN) + tail).astype(BF16).reshape(GROUP, CAP_FAR, LANES)
         )
@@ -326,7 +320,8 @@
             buffer[cell : cell + 1, :] = table[pl.ds(row, 1), :]
         total = total + bdot(buffer[...].astype(BF16)[:, :coef], leaf_far[kind], NT)
         next(tree, None)
-    total = total + result[0][:, :coef]
+        if result:
+            total = total + result.pop()[:, :coef]
     out[...] = bdot(ts[:, :coef], total.astype(BF16), NT) + near_part[...]
 
 

time: 54.6 us -> 54.8 us (level)
  no operation moved by 1% of the time
where the time goes in v3:
time: 54.8 us; the launch traced here: 54.6 us
  starting transfers between devices  26.2 us (48%)
  Pallas kernels  17.8 us (32%)
  waiting for transfers between devices  10.2 us (19%)
    ppermute x4, starting transfers between devices, shifted(): lax.ppermute(block, 'leaf', [(i, (i + by) % count) for i in range(count)])  15 us
    all_to_all x1, starting transfers between devices, body(): lax.all_to_all(far_send, 'leaf', split_axis=0, concat_axis=0, tiled=True)  11.2 us
    ppermute x4, waiting for transfers between devices, shifted(): lax.ppermute(block, 'leaf', [(i, (i + by) % count) for i in range(count)])  10.2 us
    pallas_call x1, Pallas kernels, body(): pl.pallas_call(leaf_kernel, out_shape=shape((elems, cells), F32), in_spec...  8.48 us
    pallas_call x1, Pallas kernels, body(): pl.pallas_call(send_kernel, out_shape=[shape((devices, CAP_FAR, LANES), B...  5.17 us
    pallas_call x1, Pallas kernels, body(): pl.pallas_call(tree_kernel, out_shape=[kept((index_rows, LANES), jnp.int3...  2.35 us
    pallas_call x1, Pallas kernels, body(): pl.pallas_call(near_kernel, out_shape=kept((elems, cells), F32), in_specs...  1.82 us
  transfers between devices with their start and end apart: 5, of which 2 were waited for; matrix products, arithmetic and copies ran while one was open for 0% of the time, Pallas kernels for 8%

profile of v3, /device:TPU:0, one launch (start us, length us, event | category | flops | bytes accessed | tf_op | source)
XLA Modules:
  0.0 54.6 jit_solution(7390967744864168961)
XLA Ops:
  0.0 5.2 %send.1 = (bf16[128,32,128]{2,1,0:T(8,128)(2,1)}, bf16[320,128]{1,0:T(8,128)(2,1)S(1)}, bf16[320,128]{1,0:T(8,128)(2,1)S(1)}, bf16[96,128]{1,0:T(8,128)(2,1)S(1)...) custom-call(s32[1]{0:T(128)} %bitcast.own, ...), custom_call_target="tpu_custom_call" | custom-call | tf_op jit(solution)/shard_map/send/pallas_call | solution.py:381
  5.2 0.0 copy-start.3
  5.2 0.0 copy-start.4
  5.2 0.0 copy-start.5
  5.2 11.2 %all-to-all-start = ((bf16[128,32,128]{2,1,0:T(8,128)(2,1)}), bf16[128,32,128]{2,1,0:T(8,128)(2,1)S(1)}, u32[]{:S(2)}, u32[]{:S(2)}) async-start(bf16[128,32,128]{2,1,0:T(8,128)(2,1)} %get-tuple-element.20), calls=%async_computation | async-start | bytes 2097152 | tf_op jit(solution)/shard_map/all_to_all | solution.py:411
  16.4 0.1 collective-permute-start
  16.5 7.2 %collective-permute-start.1 = (bf16[320,128]{1,0:T(8,128)(2,1)S(1)}, bf16[320,128]{1,0:T(8,128)(2,1)S(1)}, u32[]{:S(2)}, u32[]{:S(2)}) collective-permute-start(bf16[320,128]{1,0:T(8,128)(2,1)S(1)} %get-tuple-element.22), channel_id=1, source_target_pairs={{0,127},{1,0},{2,1},{3,2},{4,3},{5,4},{6,5},{7,6},{8,7},{9,8},{10,... | collective-permute-start | bytes 245768 | tf_op jit(solution)/shard_map/ppermute | solution.py:358
  23.6 0.0 copy-done.3
  23.6 0.0 copy-done.4
  23.7 0.0 copy-done.5
  23.7 2.4 %tree.1 = (s32[56,128]{1,0:T(8,128)S(1)}, f32[256,128]{1,0:T(8,128)S(1)}, bf16[128,512]{1,0:T(8,128)(2,1)S(1)}, bf16[128,1792]{1,0:T(8,128)(2,1)S(1)}) custom-call(s32[1]{0:T(128)} %bitcast.own, s32[27,256]{1,0:T(8,128)S(1)} %copy-done.5, f32[512,128]{1,0:T(8,128)S(1)} %get-tuple-element.18.agg, f32[121,2,121]{2,1,0:T(2,128)S(1)} %bitcast.5, ...), custom_call_target="tpu_custom_call" | custom-call | flops 1000000000 | bytes 1000000 | tf_op jit(solution)/shard_map/tree/pallas_call | solution.py:417
  26.0 0.0 copy-start.2
  26.0 10.1 %collective-permute-done.low = bf16[320,128]{1,0:T(8,128)(2,1)S(1)} collective-permute-done((bf16[320,128]{1,0:T(8,128)(2,1)S(1)}, bf16[320,128]{1,0:T(8,128)(2,1)S(1)}, u32[]{:S(2)}, u32[]{:S(2)}) %collective-permute-start) | collective-permute-done | bytes 81952 | tf_op jit(solution)/shard_map/ppermute | solution.py:358
  36.1 0.0 collective-permute-done.1.high
  36.2 0.1 collective-permute-start.2
  36.2 0.0 copy-start.6
  36.3 7.7 %collective-permute-start.3 = (bf16[288,128]{1,0:T(8,128)(2,1)S(1)}, bf16[288,128]{1,0:T(8,128)(2,1)S(1)}, u32[]{:S(2)}, u32[]{:S(2)}) collective-permute-start(bf16[288,128]{1,0:T(8,128)(2,1)S(1)} %pad_maximum_fusion.1), channel_id=1, source_target_pairs={{0,125},{1,126},{2,127},{3,0},{4,1},{5,2},{6,3},{7,4},{8,5},{9,6},... | collective-permute-start | bytes 221192 | tf_op jit(solution)/shard_map/ppermute | solution.py:358
  44.0 0.0 copy-done.2
  44.0 0.0 copy-done.6
  44.0 0.0 copy-start
  44.0 0.0 copy-start.1
  44.0 1.8 %near.1.near_part = f32[128,256]{1,0:T(8,128)S(1)} custom-call(s32[1]{0:T(128)} %bitcast.own, bf16[256,128]{1,0:T(8,128)(2,1)S(1)} %get-tuple-element.30.slip_rows, bf16[320,128]{1,0:T(8,128)(2,1)S(1)} %collective-permute-done.low, bf16[320,128]{1,0:T(8,128)(2,1)S(1)} %collective-permute-done.1.high, s32[9,256]{1,0:T(8,128)S(1)} %copy-done.6, ...), custom_call_target="tpu_custom_call" | custom-call | flops 1000000000 | bytes 1000000 | tf_op jit(solution)/shard_map/near/pallas_call | solution.py:435
  45.8 0.0 collective-permute-done.2.plus
  45.8 0.1 collective-permute-done.3.minus
  45.9 0.0 all-to-all-done.far
  46.0 0.0 copy-done
  46.0 0.0 copy-done.1
  46.0 8.5 %leaf.1 = f32[128,256]{1,0:T(8,128)} custom-call(s32[1]{0:T(128)} %bitcast.own, s32[56,128]{1,0:T(8,128)S(1)} %get-tuple-element.19.index_rows, bf16[128,32,128]{2,1,0:T(8,128)(2,1)S(1)} %all-to-all-done.far, bf16[320,128]{1,0:T(8,128)(2,1)S(1)} %collective-permute-done.low, bf16[320,128]{1,0:T(8,128)(2,1)S(1)} %collective-permute-done.1.high, ...), custom_call_target="tpu_custom_call" | custom-call | tf_op jit(solution)/shard_map/leaf/pallas_call | solution.py:449
  (4 shorter events, 0.0 us)
Async XLA Ops:
  5.2 18.5 %copy-start.3 = (f32[2,121,121]{2,0,1:T(2,128)S(1)}, f32[2,121,121]{2,0,1:T(2,128)}, u32[]{:S(2)}) copy-start(f32[2,121,121]{2,0,1:T(2,128)} %param.14) | copy-start | bytes 351388
  5.2 18.5 %copy-start.4 = (f32[2,121,121]{2,0,1:T(2,128)S(1)}, f32[2,121,121]{2,0,1:T(2,128)}, u32[]{:S(2)}) copy-start(f32[2,121,121]{2,0,1:T(2,128)} %param.15) | copy-start | bytes 351388
  5.2 18.4 %copy-start.5 = (s32[27,256]{1,0:T(8,128)S(1)}, s32[27,256]{1,0:T(8,128)}, u32[]{:S(2)}) copy-start(s32[27,256]{1,0:T(8,128)} %far_list.1) | copy-start | bytes 82948
  5.2 40.7 %all-to-all-start = ((bf16[128,32,128]{2,1,0:T(8,128)(2,1)}), bf16[128,32,128]{2,1,0:T(8,128)(2,1)S(1)}, u32[]{:S(2)}, u32[]{:S(2)}) async-start(bf16[128,32,128]{2,1,0:T(8,128)(2,1)} %get-tuple-element.20), calls=%async_computation | async-start | bytes 2097152 | tf_op jit(solution)/shard_map/all_to_all | solution.py:411
  16.4 19.7 %collective-permute-start = (bf16[320,128]{1,0:T(8,128)(2,1)S(1)}, bf16[320,128]{1,0:T(8,128)(2,1)S(1)}, u32[]{:S(2)}, u32[]{:S(2)}) collective-permute-start(bf16[320,128]{1,0:T(8,128)(2,1)S(1)} %get-tuple-element.21), channel_id=1, source_target_pairs={{0,1},{1,2},{2,3},{3,4},{4,5},{5,6},{6,7},{7,8},{8,9},{9,10},{10,1... | collective-permute-start | bytes 245768 | tf_op jit(solution)/shard_map/ppermute | solution.py:358
  16.5 19.6 %collective-permute-start.1 = (bf16[320,128]{1,0:T(8,128)(2,1)S(1)}, bf16[320,128]{1,0:T(8,128)(2,1)S(1)}, u32[]{:S(2)}, u32[]{:S(2)}) collective-permute-start(bf16[320,128]{1,0:T(8,128)(2,1)S(1)} %get-tuple-element.22), channel_id=1, source_target_pairs={{0,127},{1,0},{2,1},{3,2},{4,3},{5,4},{6,5},{7,6},{8,7},{9,8},{10,... | collective-permute-start | bytes 245768 | tf_op jit(solution)/shard_map/ppermute | solution.py:358
  26.0 18.0 %copy-start.2 = (bf16[9,128,128]{2,1,0:T(8,128)(2,1)S(1)}, bf16[9,128,128]{2,1,0:T(8,128)(2,1)}, u32[]{:S(2)}) copy-start(bf16[9,128,128]{2,1,0:T(8,128)(2,1)} %blocks.1) | copy-start | bytes 884740
  36.2 9.6 %collective-permute-start.2 = (bf16[288,128]{1,0:T(8,128)(2,1)S(1)}, bf16[288,128]{1,0:T(8,128)(2,1)S(1)}, u32[]{:S(2)}, u32[]{:S(2)}) collective-permute-start(bf16[288,128]{1,0:T(8,128)(2,1)S(1)} %pad_maximum_fusion), channel_id=1, source_target_pairs={{0,3},{1,4},{2,5},{3,6},{4,7},{5,8},{6,9},{7,10},{8,11},{9,12},{10... | collective-permute-start | bytes 221192 | tf_op jit(solution)/shard_map/ppermute | solution.py:358
  36.2 7.7 %copy-start.6 = (s32[9,256]{1,0:T(8,128)S(1)}, s32[9,256]{1,0:T(8,128)}, u32[]{:S(2)}) copy-start(s32[9,256]{1,0:T(8,128)} %lists.1) | copy-start | bytes 27652
  36.3 9.7 %collective-permute-start.3 = (bf16[288,128]{1,0:T(8,128)(2,1)S(1)}, bf16[288,128]{1,0:T(8,128)(2,1)S(1)}, u32[]{:S(2)}, u32[]{:S(2)}) collective-permute-start(bf16[288,128]{1,0:T(8,128)(2,1)S(1)} %pad_maximum_fusion.1), channel_id=1, source_target_pairs={{0,125},{1,126},{2,127},{3,0},{4,1},{5,2},{6,3},{7,4},{8,5},{9,6},... | collective-permute-start | bytes 221192 | tf_op jit(solution)/shard_map/ppermute | solution.py:358
  44.0 2.0 %copy-start = (bf16[27,121,121]{2,1,0:T(8,128)(2,1)S(1)}, bf16[27,121,121]{2,1,0:T(8,128)(2,1)}, u32[]{:S(2)}) copy-start(bf16[27,121,121]{2,1,0:T(8,128)(2,1)} %leaf_far.1) | copy-start | bytes 2371846
  44.0 2.0 %copy-start.1 = (bf16[128,121]{1,0:T(8,128)(2,1)S(1)}, bf16[128,121]{1,0:T(8,128)(2,1)}, u32[]{:S(2)}) copy-start(bf16[128,121]{1,0:T(8,128)(2,1)} %to_stress.1) | copy-start | bytes 92932
